TPU v7x, 32 devices: a whole 2x2x4 slice. The times are simulated.
32 devices in a mesh: row: 16 (over z, x, core), ga: 2 (over y).
Axes of the slice: x: 2, y: 2, z: 4, core: 2. Of those that a mesh axis runs over, the one named last changes fastest.
Arguments:
- pair_dens: bfloat16 [16, 256, 4096], P('row', None, 'ga'), may hold values from -0.41992188 to 0.41992188
- cond_dens: bfloat16 [16, 1024, 4096], P('row', None, 'ga'), may hold values from -0.41992188 to 0.41992188
- val_dens: bfloat16 [16, 64, 4096], P(None, None, 'row'), may hold values from -0.41992188 to 0.41992188
- screened: bfloat16 [8, 4096, 4096], P(None, 'ga', 'row'), may hold values from -1 to 6, as said below
- coulomb: bfloat16 [4096], P('ga'), may hold values from 0.29882812 to 10
- pair_list: int32 [16, 256], replicated, may hold values from 0 to 255, each once within a row
- counts: int32 [16], replicated, may hold values from 10 to 256
- q_index: int32 [16], replicated, may hold values from 0 to 7
- column_k: int32 [1], replicated, may hold values from 0 to 15
Outputs:
- kernel: bfloat16 [4096, 256], P('row', 'ga')
Inputs may be any that keep to these rules, and one draw needn't show every extreme that they name: `screened`: each diagonal entry exceeds the sum of the magnitudes of the others in its row divided by the square root of 4096 times four.
All inputs are finite; a program needn't handle non-finite values.
Results may differ from a plain program's by a relative error of at most 0.0042.
Values may be sent and summed in bfloat16 or wider, within the bound.
A program may use at most 128 MiB of HBM per device.

v0:
```python
import jax
import jax.numpy as jnp
from jax import lax
from jax.sharding import PartitionSpec as P

NV = 8
NC = 32


def broadcast(value, axis, source):
    kept = jnp.where(lax.axis_index(axis) == source, value, 0).astype(value.dtype)
    return lax.psum(kept, axis)


def per_device(
    pair_dens, cond_dens, val_dens, screened, coulomb, pair_list, counts, q_index, column_k
):
    kdev = pair_dens.shape[0]
    slots_all = pair_dens.shape[1]
    mine = lax.axis_index("row")
    column = column_k[0]
    root = column // kdev
    local_slot = column % kdev
    own_col = lax.dynamic_index_in_dim(pair_dens, local_slot, 0, keepdims=False)
    col_full = broadcast(own_col, "row", root)
    col_pairs = pair_list[column]
    col = jnp.take(col_full, col_pairs, axis=0)
    first = mine * kdev
    my_pairs = lax.dynamic_slice_in_dim(pair_list, first, kdev, 0)
    my_counts = lax.dynamic_slice_in_dim(counts, first, kdev, 0)
    blocks = jnp.take(screened, q_index, axis=0)
    screened_val = lax.psum_scatter(
        jnp.einsum("kvg,khg->kvh", val_dens, blocks, preferred_element_type=jnp.float32),
        "row",
        scatter_dimension=0,
        tiled=True,
    )
    screened_val = screened_val.astype(jnp.bfloat16)
    direct_full = jnp.einsum(
        "kag,kvg->kav", cond_dens, screened_val, preferred_element_type=jnp.float32
    )
    arranged = (
        direct_full.reshape(kdev, NC, NC, NV, NV)
        .transpose(0, 3, 1, 4, 2)
        .reshape(kdev, slots_all, slots_all)
    )
    direct = jnp.take(
        jnp.take_along_axis(arranged, my_pairs[:, :, None], axis=1), col_pairs, axis=2
    )
    rows = jnp.take_along_axis(pair_dens, my_pairs[:, :, None], axis=1)
    weighted = (rows.astype(jnp.float32) * coulomb.astype(jnp.float32)[None, None, :]).astype(
        jnp.bfloat16
    )
    exch = jnp.einsum("ksg,tg->kst", weighted, col, preferred_element_type=jnp.float32)
    slot_ids = jnp.arange(slots_all, dtype=jnp.int32)
    row_mask = (slot_ids[None, :] < my_counts[:, None]).astype(jnp.float32)
    col_mask = (slot_ids < counts[column]).astype(jnp.float32)
    masking = row_mask[:, :, None] * col_mask[None, None, :]
    combined = ((2.0 * exch - direct) * masking).reshape(kdev * slots_all, slots_all)
    summed = lax.psum_scatter(combined, "ga", scatter_dimension=1, tiled=True)
    return summed.astype(jnp.bfloat16)


def solution(mesh):
    placed = (
        P("row", None, "ga"),
        P("row", None, "ga"),
        P(None, None, "row"),
        P(None, "ga", "row"),
        P("ga"),
        P(),
        P(),
        P(),
        P(),
    )
    return jax.shard_map(
        per_device, mesh=mesh, in_specs=placed, out_specs=P("row", "ga"), check_vma=False
    )
```

profile of v0, /device:TPU:0, one launch (start us, length us, event | category | flops | bytes accessed | tf_op | source)
XLA Modules:
  0.0 245.6 jit_solution(8387644631469764746)
XLA Ops:
  6.5 0.0 copy-start
  6.5 0.0 all-reduce.2.cloned.1.call-start
  7.3 1.0 select_bitcast_fusion
  8.3 0.0 all-reduce.2.cloned.1.call-update
  8.3 0.0 reduce-scatter.3.cloned.1.call-start
  8.4 0.7 compare_select_fusion.4
  9.0 0.7 compare_and_fusion
  9.7 10.7 %gather_fusion.2 = bf16[16,2048,256]{2,1,0:T(8,128)(2,1)} fusion(bf16[8,2048,256]{2,1,0:T(8,128)(2,1)} %param.12, s32[1024]{0:T(1024)S(1)} %pad_clamp_fusion), kind=kCustom, calls=%fused_computation.2 | custom fusion | bytes 33554496 | tf_op jit(solution)/shard_map/jit(_take)/gather | solution.py:31
  20.4 0.0 copy-done
  20.4 10.8 %fusion.4 = f32[16,64,2048]{2,1,0:T(8,128)} fusion(bf16[16,64,256]{2,1,0:T(8,128)(2,1)S(1)} %copy-done, bf16[16,2048,256]{2,1,0:T(8,128)(2,1)} %gather_fusion.2, pred[16]{0:T(512)(128)(4,1)S(1)} %compare_and_fusion), kind=kOutput, calls=%fused_computation.9 | convolution fusion | flops 1082130432 | bytes 25690128 | tf_op jit(solution)/shard_map/kvg,khg->kvh/dot_general | solution.py:33
  31.2 0.0 copy-start.2
  31.2 0.0 copy-start.1
  31.2 0.0 copy-start.3
  31.2 0.0 reduce-scatter.3.cloned.1.call-update
  31.2 0.0 reduce-scatter.5.cloned.1.call-start
  31.3 0.6 copy-done.2
  31.9 0.8 compare_select_fusion.1
  32.7 0.0 copy-done.1
  32.7 1.4 gather_fusion
  34.1 0.0 copy-done.3
  34.1 0.7 fusion.20
  34.7 1.3 compare_convert_fusion
  36.1 71.2 %all-reduce.2.cloned.1.call-done = bf16[256,2048]{1,0:T(8,128)(2,1)} async-done(((bf16[256,2048]{1,0:T(8,128)(2,1)}), bf16[256,2048]{1,0:T(8,128)(2,1)}) %all-reduce.2.cloned.1.call-update) | async-done | bytes 1048592 | tf_op jit(solution)/shard_map/psum | solution.py:12
  107.3 3.7 %gather_fusion.1 = bf16[256,2048]{1,0:T(8,128)(2,1)S(1)} fusion(bf16[256,2048]{1,0:T(8,128)(2,1)} %all-reduce.2.cloned.1.call-done, s32[1024]{0:T(1024)S(1)} %pad_clamp_fusion.1), kind=kCustom, calls=%fused_computation.1 | custom fusion | bytes 2098176 | tf_op jit(solution)/shard_map/jit(_take)/gather | solution.py:27
  111.1 102.9 %reduce-scatter.3.cloned.1.call-done = f32[1,64,2048]{2,1,0:T(8,128)} async-done(((f32[16,64,2048]{2,1,0:T(8,128)}), f32[1,64,2048]{2,1,0:T(8,128)}) %reduce-scatter.3.cloned.1.call-update) | async-done | bytes 524304 | tf_op jit(solution)/shard_map/reduce_scatter | solution.py:32
  214.0 6.8 %convolution_bitcast_fusion = f32[1,8,32,8,32]{4,3,2,1,0:T(8,128)} fusion(bf16[32,32,2048,1]{2,1,0,3:T(8,128)(2,1)} %bitcast.53, f32[1,64,2048]{2,1,0:T(8,128)} %reduce-scatter.3.cloned.1.call-done), kind=kOutput, calls=%fused_computation.11 | convolution fusion | flops 268566528 | bytes 4980736 | tf_op jit(solution)/shard_map/kag,kvg->kav/dot_general | solution.py:39
  220.8 1.5 reshape.231
  222.3 1.0 gather_fusion.3
  223.3 0.1 fusion.16
  223.4 0.1 copy.12
  223.6 1.0 gather_fusion.4
  224.5 0.1 copy.13
  224.7 1.3 fusion.8
  225.9 0.0 reduce-scatter.5.cloned.1.call-update
  226.0 11.6 %reduce-scatter.5.cloned.1.call-done = f32[256,128]{1,0:T(8,128)} async-done(((f32[256,256]{1,0:T(8,128)}), f32[256,128]{1,0:T(8,128)}) %reduce-scatter.5.cloned.1.call-update) | async-done | bytes 131088 | tf_op jit(solution)/shard_map/reduce_scatter | solution.py:60
  237.5 1.5 convert_element_type.45
  (5 shorter events, 0.0 us)
Async XLA Ops:
  6.5 13.8 %copy-start = (bf16[16,64,256]{2,1,0:T(8,128)(2,1)S(1)}, bf16[16,64,256]{2,1,0:T(8,128)(2,1)}, u32[]{:S(2)}) copy-start(bf16[16,64,256]{2,1,0:T(8,128)(2,1)} %param.11) | copy-start | bytes 1572868
  6.5 100.8 %all-reduce.2.cloned.1.call-start = ((), (), s32[]{:S(2)}) async-start(), calls=%async_computation.2 | async-start | bytes 2097152 | tf_op jit(solution)/shard_map/psum | solution.py:12
  8.3 205.6 %reduce-scatter.3.cloned.1.call-start = ((), (), s32[]{:S(2)}) async-start(), calls=%async_computation.3 | async-start | bytes 8912896 | tf_op jit(solution)/shard_map/reduce_scatter | solution.py:32
  31.2 0.7 copy-start.2
  31.2 1.5 copy-start.1
  31.2 2.9 %copy-start.3 = (s32[16]{0:T(128)S(1)}, s32[16]{0:T(128)}, u32[]{:S(2)}) copy-start(s32[16]{0:T(128)} %param.15) | copy-start | bytes 196
  31.2 206.3 %reduce-scatter.5.cloned.1.call-start = ((), (), s32[]{:S(2)}) async-start(), calls=%async_computation.4 | async-start | bytes 393216 | tf_op jit(solution)/shard_map/reduce_scatter | solution.py:60
Sparse Core Ops, SparseCore 0:
  10.8 96.4 all-reduce.1
  111.4 102.5 reduce-scatter.2
  226.1 11.3 reduce-scatter.4
where the time goes:
time: 246 us
  waiting for transfers between devices  186 us (76%)
  local copies, waits for them, and re-layouts  20.7 us (8%)
  matrix products  19 us (8%)
  between operations  13.9 us (6%)
  other arithmetic  6.13 us (2%)
    reduce_scatter x1, waiting for transfers between devices, per_device(): lax.psum_scatter(jnp.einsum('kvg,khg->kvh', val_dens, blocks, preferred_e...  103 us
    psum x1, waiting for transfers between devices, broadcast(): return lax.psum(kept, axis)  71.2 us
    reduce_scatter x1, waiting for transfers between devices, per_device(): summed = lax.psum_scatter(combined, 'ga', scatter_dimension=1, tiled=True)  11.6 us
    dot_general x1, matrix products, per_device(): jnp.einsum('kvg,khg->kvh', val_dens, blocks, preferred_element_type=jnp.f...  10.8 us
    gather x1, local copies, waits for them, and re-layouts, per_device(): blocks = jnp.take(screened, q_index, axis=0)  10.7 us
    dot_general x1, matrix products, per_device(): jnp.einsum('kag,kvg->kav', cond_dens, screened_val, preferred_element_typ...  6.84 us
  transfers between devices with their start and end apart: 3, of which 3 were waited for; matrix products, arithmetic and copies ran while one was open for 13% of the time, Pallas kernels for 0%

commit v1 on v0

v1 whole, which is shorter than its diff:
```python
import functools

import jax
import jax.numpy as jnp
from jax import lax
from jax.experimental import pallas as pl
from jax.experimental.pallas import tpu as pltpu
from jax.sharding import PartitionSpec as P

NV = 8
NC = 32
BF = jnp.bfloat16
F32 = jnp.float32
MESH = pl.DeviceIdType.MESH
NT = (((1,), (1,)), ((), ()))


def split(value):
    high = value.astype(BF)
    return high, (value - high.astype(F32)).astype(BF)


def kernel(
    rows_n, ga_n, cut,
    pd_hbm, cond_hbm, val_hbm, w_hbm, coul_ref, pairs_ref, counts_ref, q_ref, column_ref,
    out_ref,
    pd, cond, val, w, part, send_a, send_b, recv_a, recv_b, send_c, recv_c, col, t_ref, kp, kr,
    load_sem, sa_s, sa_r, sb_s, sb_r, s0_s, s0_r, sc_s, sc_r, g_s, g_r, y_s, y_r,
    recv_0, send_0,
):
    r = lax.axis_index("row")
    ga = lax.axis_index("ga")
    levels = []
    while 1 << len(levels) < rows_n:
        levels.append(1 << len(levels))
    order_a = levels[1:]
    order_b = levels[2:3] + levels[1:2] + levels[3:]
    order_c = levels

    def other(index, j):
        for b in levels:
            if j & b:
                index = index + b - 2 * b * ((r // b) % 2)
        return index

    def k_of(j):
        return other(r, j)

    loads = [
        pltpu.make_async_copy(src, dst, load_sem.at[i])
        for i, (src, dst) in enumerate(
            ((pd_hbm, pd), (val_hbm, val), (w_hbm, w), (cond_hbm, cond))
        )
    ]
    for load in loads:
        load.start()

    barrier = pltpu.get_barrier_semaphore()
    for b in levels:
        pl.semaphore_signal(
            barrier, inc=1, device_id={"row": k_of(b), "ga": ga}, device_id_type=MESH
        )
    for d in range(1, ga_n):
        pl.semaphore_signal(
            barrier, inc=1, device_id={"row": r, "ga": (ga + d) % ga_n}, device_id_type=MESH
        )
    pl.semaphore_wait(barrier, len(levels) + ga_n - 1)

    started = []

    def send(src, dst, ssem, rsem, b):
        copy = pltpu.make_async_remote_copy(
            src_ref=src, dst_ref=dst, send_sem=ssem, recv_sem=rsem,
            device_id={"row": k_of(b), "ga": ga}, device_id_type=MESH,
        )
        copy.start()
        started.append(copy)
        return copy

    copies = {}

    def gather_terms(acc, name, recv, order, j):
        for b in order:
            if j & b:
                return acc, b
            copies[name, j | b].wait_recv()
            acc = acc + recv[j | b].astype(acc.dtype)
        return acc, 0

    column = column_ref[0]
    loads[0].wait()
    is_root = column == r

    def finish_c(j):
        own = pd[k_of(j)]
        own = jnp.where(is_root, own, jnp.zeros_like(own))
        acc, b = gather_terms(own, "c", recv_c, order_c, j)
        if j == 0:
            col[r] = acc
            return
        send_c[j] = acc
        copies["c", j] = send(send_c.at[j], recv_c.at[j], sc_s.at[j], sc_r.at[j], b)

    def finish(name, j):
        if name == "a":
            acc = part[j // 2, :, :cut]
            acc, b = gather_terms(acc, "a", recv_a, order_a, j)
        else:
            acc = part[j // 2, :, cut:]
            acc, b = gather_terms(acc, "b", recv_b, order_b, j)
        if j == 0:
            if name == "a":
                t_ref[:, :cut] = acc.astype(BF)
            else:
                t_ref[:, cut:] = acc.astype(BF)
            return
        if name == "a":
            send_a[j // 2] = acc.astype(BF)
            copies["a", j] = send(send_a.at[j // 2], recv_a.at[j], sa_s.at[j], sa_r.at[j], b)
        else:
            send_b[j // 2] = acc.astype(BF)
            copies["b", j] = send(send_b.at[j // 2], recv_b.at[j], sb_s.at[j], sb_r.at[j], b)

    by_depth = sorted(range(rows_n), key=lambda j: (-bin(j).count("1"), -j))

    def first_bit(order, j):
        for at, b in enumerate(order):
            if j & b:
                return at
        return len(order)

    def level(order, at, even):
        return [j for j in by_depth if (not even or j % 2 == 0) and first_bit(order, j) == at]

    for at in (0, 1):
        for j in level(order_c, at, False):
            finish_c(j)

    loads[1].wait()
    loads[2].wait()

    def partial(j):
        k = k_of(j)
        return lax.dot_general(val[k], w[q_ref[k]], NT, preferred_element_type=F32)

    evens = [j for j in by_depth if j % 2 == 0]

    def odd_step(j):
        send_0[j // 2] = partial(j).astype(BF)
        copies["0", j] = send(
            send_0.at[j // 2], recv_0.at[j // 2], s0_s.at[j // 2], s0_r.at[j // 2], 1
        )

    def even_step(j):
        value = partial(j)
        copies["0", j + 1].wait_recv()
        part[j // 2] = value + recv_0[j // 2].astype(F32)
        for name, order in (("a", order_a), ("b", order_b)):
            if first_bit(order, j) == 0:
                finish(name, j)

    skew = 2
    for step in range(len(evens) + skew):
        if step < len(evens):
            odd_step(evens[step] + 1)
        if step >= skew:
            even_step(evens[step - skew])

    for at in range(1, len(order_a)):
        for j in level(order_c, at + 1, False):
            finish_c(j)
        for name, order in (("a", order_a), ("b", order_b)):
            for j in level(order, at, True):
                finish(name, j)
    finish_c(0)

    held = [0]
    for b in reversed(levels):
        new = []
        for i in held:
            k = k_of(i)
            new.append(
                (i | b, send(col.at[k], col.at[k], g_s.at[i | b], g_r.at[i | b], b))
            )
        for i, copy in new:
            copy.wait_recv()
            held.append(i)

    slots = NV * NC
    h = pd.shape[-1]
    weighted = (pd[...].reshape(slots, h).astype(F32) * coul_ref[...].astype(F32)).astype(BF)
    exch = 2.0 * lax.dot_general(
        weighted, col[...].reshape(slots, h), NT, preferred_element_type=F32
    )
    my_pairs = pairs_ref[pl.ds(r, 1), :]
    col_pairs = pairs_ref[pl.ds(column, 1), :]
    place = lax.broadcasted_iota(jnp.int32, (slots, slots), 0)

    def pick(wanted):
        return jnp.where(place == wanted, 1.0, 0.0).astype(F32)

    rows_of = pick(my_pairs).T.astype(BF)
    rows_of_direct = pick((my_pairs % NC) * NV + my_pairs // NC).T.astype(BF)
    cols_of = pick(col_pairs).astype(BF)

    def chosen(left, value):
        high, low = split(value)
        return jnp.dot(left, high, preferred_element_type=F32) + jnp.dot(
            left, low, preferred_element_type=F32
        )

    total = chosen(rows_of, exch)

    finish("a", 0)
    finish("b", 0)
    loads[3].wait()
    vv = NV * NV
    row_id = lax.broadcasted_iota(jnp.int32, (vv, vv), 0)
    col_id = lax.broadcasted_iota(jnp.int32, (vv, vv), 1)
    swap = jnp.where(col_id == (row_id % NV) * NV + row_id // NV, 1.0, 0.0).astype(BF)
    swapped = jnp.dot(swap, t_ref[...], preferred_element_type=F32).astype(BF)
    direct = lax.dot_general(swapped, cond[...], NT, preferred_element_type=F32)
    arranged = jnp.concatenate(
        [
            jnp.concatenate(
                [
                    direct[vp * NV:(vp + 1) * NV, c * NC:(c + 1) * NC]
                    for vp in range(NV)
                ],
                axis=1,
            )
            for c in range(NC)
        ],
        axis=0,
    )
    total = total - chosen(rows_of_direct, arranged)
    high, low = split(total)
    total = jnp.dot(high, cols_of, preferred_element_type=F32) + jnp.dot(
        low, cols_of, preferred_element_type=F32
    )
    width = slots // ga_n
    for g in range(ga_n):
        kp[g] = total[:, g * width:(g + 1) * width]
    finals = []
    for d in range(1, ga_n):
        to = (ga + d) % ga_n
        copy = pltpu.make_async_remote_copy(
            src_ref=kp.at[to], dst_ref=kr.at[d - 1], send_sem=y_s.at[d - 1], recv_sem=y_r.at[d - 1],
            device_id={"row": r, "ga": to}, device_id_type=MESH,
        )
        copy.start()
        finals.append(copy)
    acc = kp[ga]
    for d, copy in enumerate(finals):
        copy.wait_recv()
        acc = acc + kr[d]
    srow = lax.broadcasted_iota(jnp.int32, (slots, width), 0)
    tcol = lax.broadcasted_iota(jnp.int32, (slots, width), 1) + ga * width
    active = (srow < counts_ref[r]) & (tcol < counts_ref[column])
    out_ref[...] = jnp.where(active, acc, 0.0).astype(BF)
    for copy in started + finals:
        copy.wait_send()


def solution(mesh):
    rows_n, ga_n = mesh.shape["row"], mesh.shape["ga"]

    def per_device(
        pair_dens, cond_dens, val_dens, screened, coulomb, pair_list, counts, q_index, column_k
    ):
        slots, h = pair_dens.shape[1:]
        vv = val_dens.shape[1]
        cut = max(128, (h * 5 // 8) // 128 * 128)
        chunk = slots // rows_n
        half = rows_n // 2
        vmem = pl.BlockSpec(memory_space=pltpu.VMEM)
        smem = pl.BlockSpec(memory_space=pltpu.SMEM)
        hbm = pl.BlockSpec(memory_space=pl.ANY)
        dma = pltpu.SemaphoreType.DMA
        return pl.pallas_call(
            functools.partial(kernel, rows_n, ga_n, cut),
            out_shape=jax.ShapeDtypeStruct((slots, slots // ga_n), BF),
            in_specs=[hbm, hbm, hbm, hbm, vmem, vmem, smem, smem, smem],
            out_specs=vmem,
            scratch_shapes=[
                pltpu.VMEM((rows_n, chunk, h), BF),
                pltpu.VMEM(cond_dens.shape[1:], BF),
                pltpu.VMEM(val_dens.shape, BF),
                pltpu.VMEM(screened.shape, BF),
                pltpu.VMEM((half, vv, h), F32),
                pltpu.VMEM((half, vv, cut), BF),
                pltpu.VMEM((half, vv, h - cut), BF),
                pltpu.VMEM((rows_n, vv, cut), BF),
                pltpu.VMEM((rows_n, vv, h - cut), BF),
                pltpu.VMEM((rows_n, chunk, h), BF),
                pltpu.VMEM((rows_n, chunk, h), BF),
                pltpu.VMEM((rows_n, chunk, h), BF),
                pltpu.VMEM((vv, h), BF),
                pltpu.VMEM((ga_n, slots, slots // ga_n), F32),
                pltpu.VMEM((max(1, ga_n - 1), slots, slots // ga_n), F32),
                dma((4,)),
                dma((rows_n,)), dma((rows_n,)),
                dma((rows_n,)), dma((rows_n,)),
                dma((half,)), dma((half,)),
                dma((rows_n,)), dma((rows_n,)),
                dma((rows_n,)), dma((rows_n,)),
                dma((max(1, ga_n - 1),)), dma((max(1, ga_n - 1),)),
                pltpu.VMEM((half, vv, h), BF),
                pltpu.VMEM((half, vv, h), BF),
            ],
            compiler_params=pltpu.CompilerParams(
                collective_id=0, has_side_effects=True, vmem_limit_bytes=60 * 1024 * 1024
            ),
        )(
            pair_dens.reshape(rows_n, chunk, h),
            cond_dens.reshape(cond_dens.shape[1:]),
            val_dens,
            screened,
            coulomb.reshape(1, h),
            pair_list,
            counts,
            q_index,
            column_k,
        )

    placed = (
        P("row", None, "ga"),
        P("row", None, "ga"),
        P(None, None, "row"),
        P(None, "ga", "row"),
        P("ga"),
        P(),
        P(),
        P(),
        P(),
    )
    return jax.shard_map(
        per_device, mesh=mesh, in_specs=placed, out_specs=P("row", "ga"), check_vma=False
    )
```

time: 246 us -> 70.9 us (0.29)
  waiting for transfers between devices: 186 us -> 0 us
  Pallas kernels: 0 us -> 67.2 us
  matrix products: 19 us -> 0 us
  local copies, waits for them, and re-layouts: 20.7 us -> 2.76 us
  between operations: 13.9 us -> 0.66 us
  other arithmetic: 6.13 us -> 0 us
    reduce_scatter x2 -> x0, waiting for transfers between devices: 114 us -> none  [the longest x1 103 us: per_device(): lax.psum_scatter(jnp.einsum('kvg,khg->kvh', val_dens, blocks, preferred_e...]
    psum x1 -> x0, waiting for transfers between devices: 71.2 us -> none  [broadcast(): return lax.psum(kept, axis)]
    pallas_call x0 -> x1, Pallas kernels: none -> 67.2 us  [per_device(): pl.pallas_call(functools.partial(kernel, rows_n, ga_n, cut), out_shape=ja...]
    dot_general x3 -> x0, matrix products: 19 us -> none  [the longest x1 10.8 us: per_device(): jnp.einsum('kvg,khg->kvh', val_dens, blocks, preferred_element_type=jnp.f...]
    gather x6 -> x0, local copies, waits for them, and re-layouts: 17.8 us -> none  [the longest x1 10.7 us: per_device(): blocks = jnp.take(screened, q_index, axis=0)]
    convert_element_type x3 -> x0, other arithmetic: 2.87 us -> none  [the longest x1 1.54 us: per_device(): return summed.astype(jnp.bfloat16)]
    select_n x4 -> x0, other arithmetic: 2.57 us -> none  [the longest x1 1.03 us: broadcast(): jnp.where(lax.axis_index(axis) == source, value, 0).astype(value.dtype)]
  transfers between devices with their start and end apart: 3 -> 0, of which waited for: 3 -> 0; matrix products, arithmetic and copies ran while one was open for 13% -> 0% of each run, Pallas kernels for 0% -> 0%
where the time goes in v1:
time: 70.9 us; the launch traced here: 70.6 us
  Pallas kernels  67.2 us (95%)
  local copies, waits for them, and re-layouts  2.76 us (4%)
    pallas_call x1, Pallas kernels, per_device(): pl.pallas_call(functools.partial(kernel, rows_n, ga_n, cut), out_shape=ja...  67.2 us
    unnamed x1, local copies, waits for them, and re-layouts  1.47 us

profile of v1, /device:TPU:0, one launch (start us, length us, event | category | flops | bytes accessed | tf_op | source)
XLA Modules:
  0.0 70.6 jit_solution(4130280025574823670)
XLA Ops:
  0.7 1.3 %reshape.11.coul_ref = bf16[1,2048]{1,0:T(2,128)(2,1)} reshape(bf16[2048]{0:T(1024)(128)(2,1)} %param.13) | data formatting | bytes 8192 | tf_op jit(solution)/shard_map/reshape | solution.py:319
  1.9 67.2 %shard_map.91 = bf16[256,128]{1,0:T(8,128)(2,1)} custom-call(bf16[16,16,2048]{2,1,0:T(8,128)(2,1)} %bitcast.3, bf16[1024,2048]{1,0:T(8,128)(2,1)} %bitcast.2, bf16[16,64,256]{2,1,0:T(8,128)(2,1)} %val_hbm.1, bf16[8,2048,256]{2,1,0:T(8,128)(2,1)} %w_hbm.1, bf16[1,2048]{1,0:T(2,128)(2,1)} %reshape.11.coul_ref, s32[16,256]{1,0:T(8,128)} %pairs_ref.1, ...), custom_call_target="tpu_custom_call" | custom-call | tf_op jit(solution)/shard_map/pallas_call | solution.py:280
  69.1 1.5 %copy.12 = bf16[256,128]{1,0:T(8,128)(2,1)} copy(bf16[256,128]{1,0:T(8,128)(2,1)} %shard_map.91) | data formatting | bytes 131072

commit v2 on v1

--- a/solution.py
+++ b/solution.py
@@ -24,17 +24,17 @@
     rows_n, ga_n, cut,
     pd_hbm, cond_hbm, val_hbm, w_hbm, coul_ref, pairs_ref, counts_ref, q_ref, column_ref,
     out_ref,
-    pd, cond, val, w, part, send_a, send_b, recv_a, recv_b, send_c, recv_c, col, t_ref, kp, kr,
-    load_sem, sa_s, sa_r, sb_s, sb_r, s0_s, s0_r, sc_s, sc_r, g_s, g_r, y_s, y_r,
-    recv_0, send_0,
+    pd, cond, val, w_a, w_b, part_a, part_b, send_a, send_b, recv_a, recv_b,
+    send_c, recv_c, col, t_a, t_b, own, kp, kr,
+    load_sem, sa_s, sa_r, sb_s, sb_r, sc_s, sc_r, g_s, g_r, y_s, y_r,
 ):
     r = lax.axis_index("row")
     ga = lax.axis_index("ga")
     levels = []
     while 1 << len(levels) < rows_n:
         levels.append(1 << len(levels))
-    order_a = levels[1:]
-    order_b = levels[2:3] + levels[1:2] + levels[3:]
+    order_a = levels
+    order_b = levels[:1] + levels[2:3] + levels[1:2] + levels[3:]
     order_c = levels
 
     def other(index, j):
@@ -49,7 +49,13 @@
     loads = [
         pltpu.make_async_copy(src, dst, load_sem.at[i])
         for i, (src, dst) in enumerate(
-            ((pd_hbm, pd), (val_hbm, val), (w_hbm, w), (cond_hbm, cond))
+            (
+                (pd_hbm, pd),
+                (val_hbm, val),
+                (w_hbm.at[:, cut:, :], w_b),
+                (w_hbm.at[:, :cut, :], w_a),
+                (cond_hbm, cond),
+            )
         )
     ]
     for load in loads:
@@ -101,25 +107,25 @@
         send_c[j] = acc
         copies["c", j] = send(send_c.at[j], recv_c.at[j], sc_s.at[j], sc_r.at[j], b)
 
-    def finish(name, j):
-        if name == "a":
-            acc = part[j // 2, :, :cut]
-            acc, b = gather_terms(acc, "a", recv_a, order_a, j)
+    streams = {
+        "a": (order_a, w_a, part_a, send_a, recv_a, sa_s, sa_r, t_a),
+        "b": (order_b, w_b, part_b, send_b, recv_b, sb_s, sb_r, t_b),
+    }
+
+    def finish(name, j, acc=None):
+        order, _, part, outgoing, recv, ssem, rsem, result = streams[name]
+        if acc is None:
+            acc, b = gather_terms(part[j // 2], name, recv, order[1:], j)
         else:
-            acc = part[j // 2, :, cut:]
-            acc, b = gather_terms(acc, "b", recv_b, order_b, j)
+            b = first_of(order, j)
         if j == 0:
-            if name == "a":
-                t_ref[:, :cut] = acc.astype(BF)
-            else:
-                t_ref[:, cut:] = acc.astype(BF)
+            result[...] = acc.astype(BF)
             return
-        if name == "a":
-            send_a[j // 2] = acc.astype(BF)
-            copies["a", j] = send(send_a.at[j // 2], recv_a.at[j], sa_s.at[j], sa_r.at[j], b)
-        else:
-            send_b[j // 2] = acc.astype(BF)
-            copies["b", j] = send(send_b.at[j // 2], recv_b.at[j], sb_s.at[j], sb_r.at[j], b)
+        outgoing[j] = acc.astype(BF)
+        copies[name, j] = send(outgoing.at[j], recv.at[j], ssem.at[j], rsem.at[j], b)
+
+    def first_of(order, j):
+        return [b for b in order if j & b][0]
 
     by_depth = sorted(range(rows_n), key=lambda j: (-bin(j).count("1"), -j))
 
@@ -136,59 +142,63 @@
         for j in level(order_c, at, False):
             finish_c(j)
 
+    evens = [j for j in by_depth if j % 2 == 0]
+
+    def partial(name, j):
+        k = k_of(j)
+        weights = streams[name][1]
+        return lax.dot_general(val[k], weights[q_ref[k]], NT, preferred_element_type=F32)
+
+    def even_step(name, j):
+        order, _, part, _, recv = streams[name][:5]
+        value = partial(name, j)
+        copies[name, j + 1].wait_recv()
+        value = value + recv[j + 1].astype(F32)
+        if j and first_of(order, j) == order[1]:
+            finish(name, j, value)
+        else:
+            part[j // 2] = value
+
+    skew = 2
     loads[1].wait()
-    loads[2].wait()
-
-    def partial(j):
-        k = k_of(j)
-        return lax.dot_general(val[k], w[q_ref[k]], NT, preferred_element_type=F32)
-
-    evens = [j for j in by_depth if j % 2 == 0]
-
-    def odd_step(j):
-        send_0[j // 2] = partial(j).astype(BF)
-        copies["0", j] = send(
-            send_0.at[j // 2], recv_0.at[j // 2], s0_s.at[j // 2], s0_r.at[j // 2], 1
-        )
-
-    def even_step(j):
-        value = partial(j)
-        copies["0", j + 1].wait_recv()
-        part[j // 2] = value + recv_0[j // 2].astype(F32)
-        for name, order in (("a", order_a), ("b", order_b)):
-            if first_bit(order, j) == 0:
-                finish(name, j)
-
-    skew = 2
-    for step in range(len(evens) + skew):
-        if step < len(evens):
-            odd_step(evens[step] + 1)
-        if step >= skew:
-            even_step(evens[step - skew])
-
-    for at in range(1, len(order_a)):
-        for j in level(order_c, at + 1, False):
-            finish_c(j)
-        for name, order in (("a", order_a), ("b", order_b)):
-            for j in level(order, at, True):
-                finish(name, j)
-    finish_c(0)
+    for name, load in (("b", 2), ("a", 3)):
+        loads[load].wait()
+        for step in range(len(evens) + skew):
+            if step < len(evens):
+                finish(name, evens[step] + 1, partial(name, evens[step] + 1))
+            if step >= skew:
+                even_step(name, evens[step - skew])
 
     held = [0]
-    for b in reversed(levels):
-        new = []
-        for i in held:
+    arriving = []
+
+    def spread(b):
+        for i, copy in arriving:
+            copy.wait_recv()
+            held.append(i)
+        arriving.clear()
+        for i in held if b else []:
             k = k_of(i)
-            new.append(
+            arriving.append(
                 (i | b, send(col.at[k], col.at[k], g_s.at[i | b], g_r.at[i | b], b))
             )
-        for i, copy in new:
-            copy.wait_recv()
-            held.append(i)
+
+    for at in range(2, len(levels)):
+        for j in level(order_c, at, False):
+            finish_c(j)
+        for one, two in zip(level(order_a, at, True), level(order_b, at, True)):
+            finish("a", one)
+            if at == len(levels) - 1:
+                finish_c(0)
+                spread(levels[-1])
+            finish("b", two)
+    for b in reversed(levels[:-1]):
+        spread(b)
+    spread(0)
 
     slots = NV * NC
     h = pd.shape[-1]
-    weighted = (pd[...].reshape(slots, h).astype(F32) * coul_ref[...].astype(F32)).astype(BF)
+    weighted = (pd[...].reshape(slots, h).astype(F32) * coul_ref[...].astype(F32).reshape(1, h)).astype(BF)
     exch = 2.0 * lax.dot_general(
         weighted, col[...].reshape(slots, h), NT, preferred_element_type=F32
     )
@@ -211,15 +221,20 @@
 
     total = chosen(rows_of, exch)
 
-    finish("a", 0)
-    finish("b", 0)
-    loads[3].wait()
     vv = NV * NV
     row_id = lax.broadcasted_iota(jnp.int32, (vv, vv), 0)
     col_id = lax.broadcasted_iota(jnp.int32, (vv, vv), 1)
     swap = jnp.where(col_id == (row_id % NV) * NV + row_id // NV, 1.0, 0.0).astype(BF)
-    swapped = jnp.dot(swap, t_ref[...], preferred_element_type=F32).astype(BF)
-    direct = lax.dot_general(swapped, cond[...], NT, preferred_element_type=F32)
+
+    def direct_of(valence, conduction):
+        swapped = jnp.dot(swap, valence, preferred_element_type=F32).astype(BF)
+        return lax.dot_general(swapped, conduction, NT, preferred_element_type=F32)
+
+    loads[4].wait()
+    finish("b", 0)
+    direct = direct_of(t_b[...], cond[:, cut:])
+    finish("a", 0)
+    direct = direct + direct_of(t_a[...], cond[:, :cut])
     arranged = jnp.concatenate(
         [
             jnp.concatenate(
@@ -240,7 +255,9 @@
     )
     width = slots // ga_n
     for g in range(ga_n):
-        kp[g] = total[:, g * width:(g + 1) * width]
+        piece = total[:, g * width:(g + 1) * width]
+        own[g] = piece
+        kp[g] = piece.astype(BF)
     finals = []
     for d in range(1, ga_n):
         to = (ga + d) % ga_n
@@ -250,10 +267,10 @@
         )
         copy.start()
         finals.append(copy)
-    acc = kp[ga]
+    acc = own[ga]
     for d, copy in enumerate(finals):
         copy.wait_recv()
-        acc = acc + kr[d]
+        acc = acc + kr[d].astype(F32)
     srow = lax.broadcasted_iota(jnp.int32, (slots, width), 0)
     tcol = lax.broadcasted_iota(jnp.int32, (slots, width), 1) + ga * width
     active = (srow < counts_ref[r]) & (tcol < counts_ref[column])
@@ -286,27 +303,28 @@
                 pltpu.VMEM((rows_n, chunk, h), BF),
                 pltpu.VMEM(cond_dens.shape[1:], BF),
                 pltpu.VMEM(val_dens.shape, BF),
-                pltpu.VMEM(screened.shape, BF),
-                pltpu.VMEM((half, vv, h), F32),
-                pltpu.VMEM((half, vv, cut), BF),
-                pltpu.VMEM((half, vv, h - cut), BF),
+                pltpu.VMEM((screened.shape[0], cut, screened.shape[2]), BF),
+                pltpu.VMEM((screened.shape[0], h - cut, screened.shape[2]), BF),
+                pltpu.VMEM((half, vv, cut), F32),
+                pltpu.VMEM((half, vv, h - cut), F32),
+                pltpu.VMEM((rows_n, vv, cut), BF),
+                pltpu.VMEM((rows_n, vv, h - cut), BF),
                 pltpu.VMEM((rows_n, vv, cut), BF),
                 pltpu.VMEM((rows_n, vv, h - cut), BF),
                 pltpu.VMEM((rows_n, chunk, h), BF),
                 pltpu.VMEM((rows_n, chunk, h), BF),
                 pltpu.VMEM((rows_n, chunk, h), BF),
-                pltpu.VMEM((vv, h), BF),
+                pltpu.VMEM((vv, cut), BF),
+                pltpu.VMEM((vv, h - cut), BF),
                 pltpu.VMEM((ga_n, slots, slots // ga_n), F32),
-                pltpu.VMEM((max(1, ga_n - 1), slots, slots // ga_n), F32),
-                dma((4,)),
+                pltpu.VMEM((ga_n, slots, slots // ga_n), BF),
+                pltpu.VMEM((max(1, ga_n - 1), slots, slots // ga_n), BF),
+                dma((5,)),
                 dma((rows_n,)), dma((rows_n,)),
                 dma((rows_n,)), dma((rows_n,)),
-                dma((half,)), dma((half,)),
                 dma((rows_n,)), dma((rows_n,)),
                 dma((rows_n,)), dma((rows_n,)),
                 dma((max(1, ga_n - 1),)), dma((max(1, ga_n - 1),)),
-                pltpu.VMEM((half, vv, h), BF),
-                pltpu.VMEM((half, vv, h), BF),
             ],
             compiler_params=pltpu.CompilerParams(
                 collective_id=0, has_side_effects=True, vmem_limit_bytes=60 * 1024 * 1024
@@ -316,7 +334,7 @@
             cond_dens.reshape(cond_dens.shape[1:]),
             val_dens,
             screened,
-            coulomb.reshape(1, h),
+            coulomb,
             pair_list,
             counts,
             q_index,

time: 70.9 us -> 64.1 us (0.904)
  Pallas kernels: 67.2 us -> 61.1 us
  local copies, waits for them, and re-layouts: 2.76 us -> 1.47 us
    pallas_call x1, Pallas kernels: 67.2 us -> 61.1 us  [per_device(): pl.pallas_call(functools.partial(kernel, rows_n, ga_n, cut), out_shape=ja...]
    reshape x1 -> x0, local copies, waits for them, and re-layouts: 1.29 us -> none  [per_device(): coulomb.reshape(1, h)]
where the time goes in v2:
time: 64.1 us; the launch traced here: 63.3 us
  Pallas kernels  61.1 us (95%)
  local copies, waits for them, and re-layouts  1.47 us (2%)
  between operations  0.66 us (1%)
    pallas_call x1, Pallas kernels, per_device(): pl.pallas_call(functools.partial(kernel, rows_n, ga_n, cut), out_shape=ja...  61.1 us
    unnamed x1, local copies, waits for them, and re-layouts  1.47 us

profile of v2, /device:TPU:0, one launch (start us, length us, event | category | flops | bytes accessed | tf_op | source)
XLA Modules:
  0.0 63.3 jit_solution(17129163959169529676)
XLA Ops:
  0.7 61.1 %shard_map.91 = bf16[256,128]{1,0:T(8,128)(2,1)} custom-call(bf16[16,16,2048]{2,1,0:T(8,128)(2,1)} %bitcast.3, bf16[1024,2048]{1,0:T(8,128)(2,1)} %bitcast.2, bf16[16,64,256]{2,1,0:T(8,128)(2,1)} %val_hbm.1, bf16[8,2048,256]{2,1,0:T(8,128)(2,1)} %w_hbm.1, bf16[2048]{0:T(1024)(128)(2,1)} %coul_ref.1, s32[16,256]{1,0:T(8,128)} %pairs_ref.1, s32[16]{0:T(128)} %counts_ref.1, ...), custom_call_target="tpu_custom_call" | custom-call | tf_op jit(solution)/shard_map/pallas_call | solution.py:297
  61.8 1.5 %copy.12 = bf16[256,128]{1,0:T(8,128)(2,1)} copy(bf16[256,128]{1,0:T(8,128)(2,1)} %shard_map.91) | data formatting | bytes 131072
